TPU v7x, 32 devices: a whole 2x2x4 slice. The times are simulated.
32 devices in a mesh: req: 2 (over core), seq: 16 (over z, y, x).
Axes of the slice: x: 2, y: 2, z: 4, core: 2. Of those that a mesh axis runs over, the one named last changes fastest.
Arguments:
- image_query: bfloat16 [256, 1536], P(('req', 'seq')), parts along dimension 0, may hold values from -6 to 6
- image_key: bfloat16 [256, 1536], P(('req', 'seq')), parts along dimension 0, may hold values from -6 to 6
- image_value: bfloat16 [256, 1536], P(('req', 'seq')), parts along dimension 0, may hold values from -6 to 6
- text_query: bfloat16 [1024, 1536], P('req'), parts along dimension 0, may hold values from -6 to 6
- text_key: bfloat16 [1024, 1536], P('req'), parts along dimension 0, may hold values from -6 to 6
- text_value: bfloat16 [1024, 1536], P('req'), parts along dimension 0, may hold values from -6 to 6
- image_query_gain: float32 [128], replicated, may hold values from 1 to 8
- image_key_gain: float32 [128], replicated, may hold values from 1 to 8
- text_query_gain: float32 [128], replicated, may hold values from 1 to 2.5
- text_key_gain: float32 [128], replicated, may hold values from 1 to 2.5
- image_order: int32 [256], P(('req', 'seq')), parts along dimension 0, may hold values from 0 to 127, each once
- text_length: int32 [2], P('req'), parts along dimension 0, may hold values from 256 to 512
Outputs:
- image_out: bfloat16 [256, 1536], P(('req', 'seq')), parts along dimension 0
- text_out: bfloat16 [1024, 1536], P(('req', 'seq')), parts along dimension 0
There are 2 independent parts, one for each index of `req`. A program takes and returns all parts, laid end to end along the dimension named above; an argument that names none is the same for every part. Nothing has to cross between parts.
Inputs may be any that keep to these rules, and one draw needn't show every extreme that they name: `image_order`: every position 0 to 127 appears once.
All inputs are finite; a program needn't handle non-finite values.
Results may differ from a plain program's by a relative error of at most 0.005.
The roundings to bfloat16 on the way count: a program that leaves them out, or rounds other values in their place, can miss the bound.
Values may be sent and summed in bfloat16 or wider, within the bound.
A program may use at most 64 MiB of HBM per device.

v0:
```python
import functools
import math

import jax
import jax.numpy as jnp
from jax import lax
from jax.experimental import pallas as pl
from jax.experimental.pallas import tpu as pltpu
from jax.sharding import PartitionSpec as P

GRID_W = 64
EPS = 1e-06
LOW = -1e30
MESH = pl.DeviceIdType.MESH


def line_sizes(devices):
    z_size = 4 if devices % 4 == 0 else 1
    rest = devices // z_size
    x_size = 1
    while x_size * x_size * 4 <= rest and rest % (x_size * 2) == 0:
        x_size *= 2
    return z_size, rest // x_size, x_size


def rsqrt_mean(values):
    return lax.rsqrt(jnp.mean(values * values, axis=-1, keepdims=True) + EPS)


def kernel(
    devices,
    iq_ref,
    ik_ref,
    iv_ref,
    tq_ref,
    tk_ref,
    tv_ref,
    iqg_ref,
    ikg_ref,
    tqg_ref,
    tkg_ref,
    order_ref,
    length_ref,
    io_ref,
    to_ref,
    kbuf,
    vbuf,
    tq_buf,
    tk_buf,
    tv_buf,
    qs,
    m_buf,
    l_buf,
    o_buf,
    recv_sem,
    send_sem,
    local_sem,
):
    zs, ys, xs = line_sizes(devices)
    me = lax.axis_index("seq")
    req = lax.axis_index("req")
    x_me = me % xs
    y_me = (me // xs) % ys
    z_me = me // (xs * ys)

    def block(z, y, x):
        return (z * ys + y) * xs + x

    if zs == 4:
        z_others = [z_me + 1 - 2 * (z_me % 2), 3 - z_me, (z_me + 2) % 4]
    else:
        z_others = []
    y_others = [(y_me + d) % ys for d in range(1, ys)]
    x_others = [(x_me + d) % xs for d in range(1, xs)]
    z_peers = [block(z, y_me, x_me) for z in z_others]
    y_peers = [block(z_me, y, x_me) for y in y_others]
    x_peers = [block(z_me, y_me, x) for x in x_others]
    peers = z_peers + y_peers + x_peers

    barrier = pltpu.get_barrier_semaphore()
    for peer in peers:
        pl.semaphore_signal(barrier, inc=1, device_id=(req, peer), device_id_type=MESH)

    own_rows, width = iq_ref.shape
    size = iqg_ref.shape[-1]
    heads = width // size
    share = tq_buf.shape[0]
    text_rows = tk_ref.shape[0]
    rows = share + own_rows
    groups = tk_buf.shape[0]
    per = heads // groups
    span = per * size
    scale = math.log2(math.e) / math.sqrt(size)

    tq_copy = pltpu.make_async_copy(
        tq_ref.at[pl.ds(pl.multiple_of(me * share, share), share), :],
        tq_buf,
        local_sem.at[2 * groups],
    )
    tq_copy.start()
    text_copies = []
    for g in range(groups):
        pair = (
            pltpu.make_async_copy(
                tk_ref.at[:, pl.ds(g * span, span)], tk_buf.at[g], local_sem.at[2 * g]
            ),
            pltpu.make_async_copy(
                tv_ref.at[:, pl.ds(g * span, span)], tv_buf.at[g], local_sem.at[2 * g + 1]
            ),
        )
        for copy in pair:
            copy.start()
        text_copies.append(pair)

    half_length = own_rows * devices // 2
    lane = lax.broadcasted_iota(jnp.int32, (own_rows, size), 1)
    row = lax.broadcasted_iota(jnp.int32, (own_rows, size), 0)
    pair_id = lane // 2
    first = pair_id < 8
    second = pair_id < 36
    coordinate = jnp.zeros((own_rows, size), jnp.int32)
    for r in range(own_rows):
        position = order_ref[r]
        inside = position % half_length
        here = jnp.where(
            first,
            position // half_length,
            jnp.where(second, inside // GRID_W, inside % GRID_W),
        )
        coordinate = jnp.where(row == r, here, coordinate)
    within = jnp.where(first, pair_id, jnp.where(second, pair_id - 8, pair_id - 36))
    step = jnp.where(first, 2.0 / 16.0, 2.0 / 56.0) * (-math.log(10000.0))
    angle = coordinate.astype(jnp.float32) * jnp.exp(within.astype(jnp.float32) * step)
    cosine = jnp.cos(angle)
    sine = jnp.sin(angle)
    even = lane % 2 == 0
    sine = jnp.where(even, -sine, sine)

    def turned(values, gain):
        normed = values * rsqrt_mean(values) * gain
        swapped = jnp.where(
            even, pltpu.roll(normed, size - 1, 1), pltpu.roll(normed, 1, 1)
        )
        return normed * cosine + swapped * sine

    for h in range(heads):
        cols = slice(h * size, (h + 1) * size)
        key = turned(ik_ref[:, cols].astype(jnp.float32), ikg_ref[...])
        kbuf[me, :, cols] = key.astype(jnp.bfloat16)
    vbuf[me] = iv_ref[...]

    pl.semaphore_wait(barrier, len(peers))

    count = [0]
    sends = []

    def send(kind, idx, peer, source=None):
        buf = (kbuf, vbuf)[kind]
        copy = pltpu.make_async_remote_copy(
            src_ref=buf.at[idx] if source is None else source,
            dst_ref=buf.at[idx],
            send_sem=send_sem.at[count[0]],
            recv_sem=recv_sem.at[kind, idx],
            device_id=(req, peer),
            device_id_type=MESH,
        )
        count[0] += 1
        copy.start()
        sends.append(copy)

    def arrive(kind, idx):
        buf = (kbuf, vbuf)[kind]
        pltpu.make_async_remote_copy(
            src_ref=buf.at[idx],
            dst_ref=buf.at[idx],
            send_sem=send_sem.at[0],
            recv_sem=recv_sem.at[kind, idx],
            device_id=(req, me),
            device_id_type=MESH,
        ).wait_recv()

    for group in (z_peers, y_peers, x_peers):
        for peer in group:
            send(1, me, peer, iv_ref)
            send(0, me, peer)

    def near_plane():
        for y in y_others:
            idx = block(z_me, y, x_me)
            arrive(0, idx)
            for peer in x_peers:
                send(0, idx, peer)
        for x in x_others:
            idx = block(z_me, y_me, x)
            arrive(1, idx)
            for peer in y_peers:
                send(1, idx, peer)

    def far_column(z):
        idx = block(z, y_me, x_me)
        for kind in (0, 1):
            arrive(kind, idx)
            for peer in y_peers + x_peers:
                send(kind, idx, peer)

    def far_plane(z):
        for y in y_others:
            idx = block(z, y, x_me)
            arrive(0, idx)
            for peer in x_peers:
                send(0, idx, peer)
        for x in x_others:
            idx = block(z, y_me, x)
            arrive(1, idx)
            for peer in y_peers:
                send(1, idx, peer)

    stages = [[] for _ in range(groups)]
    tasks = [near_plane]
    tasks += [functools.partial(far_column, z) for z in z_others]
    tasks += [functools.partial(far_plane, z) for z in z_others]
    for i, task in enumerate(tasks):
        stages[min(i * groups // len(tasks), groups - 1)].append(task)

    tq_copy.wait()
    for h in range(heads):
        cols = slice(h * size, (h + 1) * size)
        text = tq_buf[:, cols].astype(jnp.float32)
        text = text * rsqrt_mean(text) * tqg_ref[...]
        image = turned(iq_ref[:, cols].astype(jnp.float32), iqg_ref[...])
        qs[h] = jnp.concatenate([text, image], axis=0).astype(jnp.bfloat16)

    valid = lax.broadcasted_iota(jnp.int32, (rows, text_rows), 1) < length_ref[0]

    def scores_of(query, key):
        return (
            lax.dot_general(
                query, key, (((1,), (1,)), ((), ())), preferred_element_type=jnp.float32
            )
            * scale
        )

    for g in range(groups):
        for copy in text_copies[g]:
            copy.wait()
        for i in range(per):
            h = g * per + i
            cols = slice(i * size, (i + 1) * size)
            key = tk_buf[g, :, cols].astype(jnp.float32)
            key = (key * rsqrt_mean(key) * tkg_ref[...]).astype(jnp.bfloat16)
            scores = jnp.where(valid, scores_of(qs[h], key), LOW)
            top = jnp.max(scores, axis=-1, keepdims=True)
            expo = jnp.where(valid, jnp.exp2(scores - top), 0.0)
            m_buf[h] = jnp.broadcast_to(top, (rows, size))
            l_buf[h] = jnp.broadcast_to(jnp.sum(expo, axis=-1, keepdims=True), (rows, size))
            o_buf[h] = jnp.dot(
                expo.astype(jnp.bfloat16),
                tv_buf[g, :, cols],
                preferred_element_type=jnp.float32,
            )
        for task in stages[g]:
            task()

    for z in [z_me] + z_others:
        for y in [y_me] + y_others:
            for x in x_others:
                arrive(0, block(z, y, x))
        for x in [x_me] + x_others:
            for y in y_others:
                arrive(1, block(z, y, x))

    def lanes(h):
        return slice(h * size, (h + 1) * size)

    def gathered(buf, h):
        whole = buf[:, :, lanes(h)].astype(jnp.float32)
        return whole.reshape(devices * own_rows, size).astype(jnp.bfloat16)

    every = range(heads)
    scores = [scores_of(qs[h], gathered(kbuf, h)) for h in every]
    olds = [m_buf[h] for h in every]
    tops = [
        jnp.maximum(olds[h][:, :1], jnp.max(scores[h], axis=-1, keepdims=True))
        for h in every
    ]
    expos = [jnp.exp2(scores[h] - tops[h]) for h in every]
    added = [
        jnp.dot(
            expos[h].astype(jnp.bfloat16),
            gathered(vbuf, h),
            preferred_element_type=jnp.float32,
        )
        for h in every
    ]
    sums = [jnp.sum(expos[h], axis=-1, keepdims=True) for h in every]
    for h in every:
        back = jnp.exp2(olds[h] - tops[h])
        out = (o_buf[h] * back + added[h]) / (l_buf[h] * back + sums[h])
        to_ref[:, lanes(h)] = out[:share].astype(jnp.bfloat16)
        io_ref[:, lanes(h)] = out[share:].astype(jnp.bfloat16)

    for copy in sends:
        copy.wait_send()


def send_count(devices):
    zs, ys, xs = line_sizes(devices)
    keys = (zs - 1) + zs * (ys - 1) + zs * ys * (xs - 1)
    values = (zs - 1) + zs * (xs - 1) + zs * xs * (ys - 1)
    return keys + values


def local(iq, ik, iv, tq, tk, tv, iqg, ikg, tqg, tkg, order, length):
    devices = lax.axis_size("seq")
    own_rows, width = iq.shape
    size = iqg.shape[0]
    heads = width // size
    text_rows = tq.shape[0]
    share = text_rows // devices
    rows = share + own_rows
    groups = heads // 2 if heads % 2 == 0 else heads
    span = width // groups
    vmem = pl.BlockSpec(memory_space=pltpu.VMEM)
    smem = pl.BlockSpec(memory_space=pltpu.SMEM)
    hbm = pl.BlockSpec(memory_space=pl.ANY)
    gains = [g.reshape(1, size) for g in (iqg, ikg, tqg, tkg)]
    return pl.pallas_call(
        functools.partial(kernel, devices),
        out_shape=(
            jax.ShapeDtypeStruct((own_rows, width), jnp.bfloat16),
            jax.ShapeDtypeStruct((share, width), jnp.bfloat16),
        ),
        in_specs=[vmem] * 3 + [hbm] * 3 + [vmem] * 4 + [smem] * 2,
        out_specs=(vmem, vmem),
        scratch_shapes=[
            pltpu.VMEM((devices, own_rows, width), jnp.bfloat16),
            pltpu.VMEM((devices, own_rows, width), jnp.bfloat16),
            pltpu.VMEM((share, width), jnp.bfloat16),
            pltpu.VMEM((groups, text_rows, span), jnp.bfloat16),
            pltpu.VMEM((groups, text_rows, span), jnp.bfloat16),
            pltpu.VMEM((heads, rows, size), jnp.bfloat16),
            pltpu.VMEM((heads, rows, size), jnp.float32),
            pltpu.VMEM((heads, rows, size), jnp.float32),
            pltpu.VMEM((heads, rows, size), jnp.float32),
            pltpu.SemaphoreType.DMA((2, devices)),
            pltpu.SemaphoreType.DMA((send_count(devices),)),
            pltpu.SemaphoreType.DMA((2 * groups + 1,)),
        ],
        compiler_params=pltpu.CompilerParams(
            collective_id=0, has_side_effects=True, vmem_limit_bytes=62 * 1024 * 1024
        ),
    )(iq, ik, iv, tq, tk, tv, *gains, order, length)


def solution(mesh):
    rows = P(("req", "seq"), None)
    text = P("req", None)
    return jax.shard_map(
        local,
        mesh=mesh,
        in_specs=(rows, rows, rows, text, text, text)
        + (P(), P(), P(), P(), P(("req", "seq")), P("req")),
        out_specs=(rows, rows),
        check_vma=False,
    )
```

profile of v0, /device:TPU:0, one launch (start us, length us, event | category | flops | bytes accessed | tf_op | source)
XLA Modules:
  0.0 24.7 jit_solution(7121149123985609131)
XLA Ops:
  1.3 20.5 %shard_map.131 = (bf16[8,1536]{1,0:T(8,128)(2,1)}, bf16[32,1536]{1,0:T(8,128)(2,1)}) custom-call(bf16[8,1536]{1,0:T(8,128)(2,1)} %iq_ref.1, bf16[8,1536]{1,0:T(8,128)(2,1)} %ik_ref.1, bf16[8,1536]{1,0:T(8,128)(2,1)} %iv_ref.1, bf16[512,1536]{1,0:T(8,128)(2,1)} %tq_ref.1, bf16[512,1536]{1,0:T(8,128)(2,1)} %tk_ref.1, bf16[512,1536]{1,0:T(8,128)(2,1)} %tv_ref.1, ...), custom_call_target="tpu_custom_call" | custom-call | tf_op jit(solution)/shard_map/pallas_call | solution.py:327
  21.8 1.3 %copy.17 = bf16[8,1536]{1,0:T(8,128)(2,1)} copy(bf16[8,1536]{1,0:T(8,128)(2,1)} %get-tuple-element.4) | data formatting | bytes 49152
  23.1 1.5 %copy.18 = bf16[32,1536]{1,0:T(8,128)(2,1)} copy(bf16[32,1536]{1,0:T(8,128)(2,1)} %get-tuple-element.5) | data formatting | bytes 196608
where the time goes:
time: 24.9 us; the launch traced here: 24.7 us
  Pallas kernels  20.5 us (82%)
  local copies, waits for them, and re-layouts  2.89 us (12%)
  between operations  1.29 us (5%)
    pallas_call x1, Pallas kernels, local(): pl.pallas_call(functools.partial(kernel, devices), out_shape=(jax.ShapeDt...  20.5 us
    unnamed x2, local copies, waits for them, and re-layouts  2.89 us

commit v1 on v0

v1 whole, which is shorter than its diff:
```python
import functools
import math

import jax
import jax.numpy as jnp
from jax import lax
from jax.experimental import pallas as pl
from jax.experimental.pallas import tpu as pltpu
from jax.sharding import PartitionSpec as P

GRID_W = 64
EPS = 1e-06
LOW = -1e30
TEAM = 4
MESH = pl.DeviceIdType.MESH


def rsqrt_mean(values):
    return lax.rsqrt(jnp.mean(values * values, axis=-1, keepdims=True) + EPS)


def kernel(
    devices,
    iq_ref,
    ik_ref,
    iv_ref,
    tq_ref,
    tk_ref,
    tv_ref,
    iqg_ref,
    ikg_ref,
    tqg_ref,
    tkg_ref,
    order_ref,
    length_ref,
    out_ref,
    iq_buf,
    ik_buf,
    iv_buf,
    tq_buf,
    tk_buf,
    tv_buf,
    gain_buf,
    order_buf,
    length_buf,
    kv_own,
    q_own,
    kv_all,
    q_team,
    qs,
    m_buf,
    l_buf,
    o_buf,
    back_own,
    back_all,
    local_sem,
    kv_send,
    kv_recv,
    q_send,
    q_recv,
    back_send,
    back_recv,
):
    me = lax.axis_index("seq")
    req = lax.axis_index("req")
    seat = me % TEAM
    team = me // TEAM
    mates = [(team * TEAM + (seat ^ k), seat ^ k) for k in (3, 2, 1)]

    barrier = pltpu.get_barrier_semaphore()
    for d in range(1, devices):
        pl.semaphore_signal(
            barrier, inc=1, device_id=(req, (me + d) % devices), device_id_type=MESH
        )

    own_rows, width = iq_buf.shape
    size = gain_buf.shape[-1]
    heads = width // size
    text_rows, span = tk_buf.shape
    per = span // size
    team_text = tq_buf.shape[0]
    share = team_text // TEAM
    team_rows = team_text + TEAM * own_rows
    scale = math.log2(math.e) / math.sqrt(size)

    lanes = pl.ds(pl.multiple_of(seat * span, span), span)
    text = pl.ds(pl.multiple_of(team * team_text, team_text), team_text)
    loads = []
    for src, dst in (
        (order_ref, order_buf),
        (ik_ref, ik_buf),
        (ikg_ref, gain_buf.at[0]),
        (iv_ref, iv_buf),
        (iq_ref, iq_buf),
        (iqg_ref, gain_buf.at[1]),
        (tk_ref.at[:, lanes], tk_buf),
        (tkg_ref, gain_buf.at[2]),
        (tq_ref.at[text, lanes], tq_buf),
        (tqg_ref, gain_buf.at[3]),
        (length_ref, length_buf),
        (tv_ref.at[:, lanes], tv_buf),
    ):
        copy = pltpu.make_async_copy(src, dst, local_sem.at[len(loads)])
        copy.start()
        loads.append(copy)

    loads[0].wait()
    half_length = own_rows * devices // 2
    lane = lax.broadcasted_iota(jnp.int32, (own_rows, size), 1)
    row = lax.broadcasted_iota(jnp.int32, (own_rows, size), 0)
    pair_id = lane // 2
    first = pair_id < 8
    second = pair_id < 36
    coordinate = jnp.zeros((own_rows, size), jnp.int32)
    for r in range(own_rows):
        position = order_buf[r]
        inside = position % half_length
        here = jnp.where(
            first,
            position // half_length,
            jnp.where(second, inside // GRID_W, inside % GRID_W),
        )
        coordinate = jnp.where(row == r, here, coordinate)
    within = jnp.where(first, pair_id, jnp.where(second, pair_id - 8, pair_id - 36))
    step = jnp.where(first, 2.0 / 16.0, 2.0 / 56.0) * (-math.log(10000.0))
    angle = coordinate.astype(jnp.float32) * jnp.exp(within.astype(jnp.float32) * step)
    cosine = jnp.cos(angle)
    sine = jnp.sin(angle)
    even = lane % 2 == 0
    sine = jnp.where(even, -sine, sine)

    def turned(values, gain):
        normed = values * rsqrt_mean(values) * gain
        swapped = jnp.where(
            even, pltpu.roll(normed, size - 1, 1), pltpu.roll(normed, 1, 1)
        )
        return normed * cosine + swapped * sine

    for i in (1, 2, 3):
        loads[i].wait()
    for h in range(heads):
        wide = slice(h * size, (h + 1) * size)
        cols = slice(h % per * size, (h % per + 1) * size)
        key = turned(ik_buf[:, wide].astype(jnp.float32), gain_buf[0])
        both = jnp.concatenate([key, iv_buf[:, wide].astype(jnp.float32)], axis=0)
        kv_own[h // per, :, cols] = both.astype(jnp.bfloat16)
    for i in (4, 5):
        loads[i].wait()
    for h in range(heads):
        wide = slice(h * size, (h + 1) * size)
        cols = slice(h % per * size, (h % per + 1) * size)
        query = turned(iq_buf[:, wide].astype(jnp.float32), gain_buf[1])
        q_own[h // per, :, cols] = query.astype(jnp.bfloat16)
    kv_all[me] = kv_own[seat]
    q_team[seat] = q_own[seat]

    pl.semaphore_wait(barrier, devices - 1)

    def remote(src, dst, send, recv, peer):
        return pltpu.make_async_remote_copy(
            src_ref=src,
            dst_ref=dst,
            send_sem=send,
            recv_sem=recv,
            device_id=(req, peer),
            device_id_type=MESH,
        )

    def kv_copy(peer, origin):
        return remote(
            kv_own.at[peer % TEAM],
            kv_all.at[origin],
            kv_send.at[peer],
            kv_recv.at[origin],
            peer,
        )

    def q_copy(peer, mate, origin):
        return remote(
            q_own.at[mate], q_team.at[origin], q_send.at[mate], q_recv.at[origin], peer
        )

    def back_copy(peer, mate, origin):
        return remote(
            back_own.at[mate],
            back_all.at[origin],
            back_send.at[mate],
            back_recv.at[origin],
            peer,
        )

    for t in range(devices // TEAM):
        for k in (3, 2, 1, 0):
            peer = t * TEAM + (seat ^ k)

            @pl.when(peer != me)
            def _():
                kv_copy(peer, me).start()

    for peer, mate in mates:
        q_copy(peer, mate, seat).start()

    for i in range(6, 12):
        loads[i].wait()

    column = lax.broadcasted_iota(jnp.int32, (1, text_rows), 1)
    bias = jnp.where(column < length_buf[0], 0.0, LOW)

    def scores_of(query, key):
        return (
            lax.dot_general(
                query, key, (((1,), (1,)), ((), ())), preferred_element_type=jnp.float32
            )
            * scale
        )

    def text_part(h, rows, query):
        cols = slice(h * size, (h + 1) * size)
        count = query.shape[0]
        scores = scores_of(query, tk_buf[:, cols]) + bias
        top = jnp.max(scores, axis=-1, keepdims=True)
        expo = jnp.exp2(scores - top)
        total = jnp.sum(expo, axis=-1, keepdims=True)
        m_buf[h, rows] = jnp.broadcast_to(top, (count, size))
        l_buf[h, rows] = jnp.broadcast_to(total, (count, size))
        o_buf[h, rows] = jnp.dot(
            expo.astype(jnp.bfloat16),
            tv_buf[:, cols],
            preferred_element_type=jnp.float32,
        )

    for h in range(per):
        cols = slice(h * size, (h + 1) * size)
        key = tk_buf[:, cols].astype(jnp.float32)
        tk_buf[:, cols] = (key * rsqrt_mean(key) * gain_buf[2]).astype(jnp.bfloat16)
        query = tq_buf[:, cols].astype(jnp.float32)
        query = (query * rsqrt_mean(query) * gain_buf[3]).astype(jnp.bfloat16)
        qs[h, :team_text] = query
        text_part(h, slice(0, team_text), query)

    for peer, mate in mates:
        q_copy(me, mate, mate).wait_recv()
    for h in range(per):
        cols = slice(h * size, (h + 1) * size)
        query = q_team[:, :, cols].astype(jnp.float32)
        query = query.reshape(TEAM * own_rows, size).astype(jnp.bfloat16)
        qs[h, team_text:] = query
        text_part(h, slice(team_text, team_rows), query)

    for d in range(1, devices):
        kv_copy(me, (me + d) % devices).wait_recv()

    def gathered(start, h):
        cols = slice(h * size, (h + 1) * size)
        whole = kv_all[:, start : start + own_rows, cols].astype(jnp.float32)
        return whole.reshape(devices * own_rows, size).astype(jnp.bfloat16)

    every = range(per)
    scores = [scores_of(qs[h], gathered(0, h)) for h in every]
    olds = [m_buf[h] for h in every]
    tops = [
        jnp.maximum(olds[h][:, :1], jnp.max(scores[h], axis=-1, keepdims=True))
        for h in every
    ]
    expos = [jnp.exp2(scores[h] - tops[h]) for h in every]
    added = [
        jnp.dot(
            expos[h].astype(jnp.bfloat16),
            gathered(own_rows, h),
            preferred_element_type=jnp.float32,
        )
        for h in every
    ]
    sums = [jnp.sum(expos[h], axis=-1, keepdims=True) for h in every]
    for h in every:
        cols = slice(h * size, (h + 1) * size)
        back = jnp.exp2(olds[h] - tops[h])
        out = (o_buf[h] * back + added[h]) / (l_buf[h] * back + sums[h])
        for s in range(TEAM):
            part = jnp.concatenate(
                [
                    out[s * share : (s + 1) * share],
                    out[team_text + s * own_rows : team_text + (s + 1) * own_rows],
                ],
                axis=0,
            )
            back_own[s, :, cols] = part.astype(jnp.bfloat16)
    for peer, mate in mates:
        back_copy(peer, mate, seat).start()
    back_all[seat] = back_own[seat]
    for peer, mate in mates:
        back_copy(me, mate, mate).wait_recv()
    out_ref[...] = back_all[...]

    for d in range(1, devices):
        kv_copy((me + d) % devices, me).wait_send()
    for peer, mate in mates:
        q_copy(peer, mate, seat).wait_send()
        back_copy(peer, mate, seat).wait_send()


def spread(parts_ref, io_ref, to_ref):
    share = to_ref.shape[0]
    span = parts_ref.shape[-1]
    for s in range(TEAM):
        cols = slice(s * span, (s + 1) * span)
        to_ref[:, cols] = parts_ref[s, :share]
        io_ref[:, cols] = parts_ref[s, share:]


def local(iq, ik, iv, tq, tk, tv, iqg, ikg, tqg, tkg, order, length):
    devices = lax.axis_size("seq")
    own_rows, width = iq.shape
    size = iqg.shape[0]
    span = width // TEAM
    per = span // size
    text_rows = tq.shape[0]
    share = text_rows // devices
    team_text = share * TEAM
    team_rows = team_text + TEAM * own_rows
    vmem = pl.BlockSpec(memory_space=pltpu.VMEM)
    hbm = pl.BlockSpec(memory_space=pl.ANY)
    gains = [g.reshape(1, size) for g in (iqg, ikg, tqg, tkg)]
    bf16, f32 = jnp.bfloat16, jnp.float32
    parts = pl.pallas_call(
        functools.partial(kernel, devices),
        out_shape=pltpu.VMEM((TEAM, share + own_rows, span), bf16),
        in_specs=[hbm] * 12,
        out_specs=vmem,
        scratch_shapes=[
            pltpu.VMEM((own_rows, width), bf16),
            pltpu.VMEM((own_rows, width), bf16),
            pltpu.VMEM((own_rows, width), bf16),
            pltpu.VMEM((team_text, span), bf16),
            pltpu.VMEM((text_rows, span), bf16),
            pltpu.VMEM((text_rows, span), bf16),
            pltpu.VMEM((4, 1, size), f32),
            pltpu.SMEM((own_rows,), jnp.int32),
            pltpu.SMEM((1,), jnp.int32),
            pltpu.VMEM((TEAM, 2 * own_rows, span), bf16),
            pltpu.VMEM((TEAM, own_rows, span), bf16),
            pltpu.VMEM((devices, 2 * own_rows, span), bf16),
            pltpu.VMEM((TEAM, own_rows, span), bf16),
            pltpu.VMEM((per, team_rows, size), bf16),
            pltpu.VMEM((per, team_rows, size), f32),
            pltpu.VMEM((per, team_rows, size), f32),
            pltpu.VMEM((per, team_rows, size), f32),
            pltpu.VMEM((TEAM, share + own_rows, span), bf16),
            pltpu.VMEM((TEAM, share + own_rows, span), bf16),
            pltpu.SemaphoreType.DMA((12,)),
            pltpu.SemaphoreType.DMA((devices,)),
            pltpu.SemaphoreType.DMA((devices,)),
            pltpu.SemaphoreType.DMA((TEAM,)),
            pltpu.SemaphoreType.DMA((TEAM,)),
            pltpu.SemaphoreType.DMA((TEAM,)),
            pltpu.SemaphoreType.DMA((TEAM,)),
        ],
        compiler_params=pltpu.CompilerParams(
            collective_id=0, has_side_effects=True, vmem_limit_bytes=32 * 1024 * 1024
        ),
    )(iq, ik, iv, tq, tk, tv, *gains, order, length)
    parts = pltpu.with_memory_space_constraint(parts, pltpu.VMEM)
    return pl.pallas_call(
        spread,
        out_shape=(
            jax.ShapeDtypeStruct((own_rows, width), bf16),
            jax.ShapeDtypeStruct((share, width), bf16),
        ),
        in_specs=[vmem],
        out_specs=(vmem, vmem),
    )(parts)


def solution(mesh):
    rows = P(("req", "seq"), None)
    text = P("req", None)
    return jax.shard_map(
        local,
        mesh=mesh,
        in_specs=(rows, rows, rows, text, text, text)
        + (P(), P(), P(), P(), P(("req", "seq")), P("req")),
        out_specs=(rows, rows),
        check_vma=False,
    )
```

time: 24.9 us -> 28.2 us (1.13)
  local copies, waits for them, and re-layouts: 2.89 us -> 9.7 us
  Pallas kernels: 20.5 us -> 16.7 us
    unnamed x2 -> x22, local copies, waits for them, and re-layouts: 2.89 us -> 9.7 us
    pallas_call x1 -> x2, Pallas kernels: 20.5 us -> 16.7 us  [the longest x1 16.1 us: local(): pl.pallas_call(functools.partial(kernel, devices), out_shape=pltpu.VMEM((...]
where the time goes in v1:
time: 28.2 us; the launch traced here: 27.7 us
  Pallas kernels  16.7 us (59%)
  local copies, waits for them, and re-layouts  9.7 us (34%)
  between operations  1.31 us (5%)
    pallas_call x1, Pallas kernels, local(): pl.pallas_call(functools.partial(kernel, devices), out_shape=pltpu.VMEM((...  16.1 us
    unnamed x22, local copies, waits for them, and re-layouts  9.7 us
    pallas_call x1, Pallas kernels, local(): pl.pallas_call(spread, out_shape=(jax.ShapeDtypeStruct((own_rows, width),...  0.65 us

profile of v1, /device:TPU:0, one launch (start us, length us, event | category | flops | bytes accessed | tf_op | source)
XLA Modules:
  0.0 27.7 jit_solution(10750973345406700630)
XLA Ops:
  1.3 0.0 copy-start
  1.3 1.4 %copy-done = bf16[512,1536]{1,0:T(8,128)(2,1)S(1)} copy-done((bf16[512,1536]{1,0:T(8,128)(2,1)S(1)}, bf16[512,1536]{1,0:T(8,128)(2,1)}, u32[]{:S(2)}) %copy-start) | copy-done | bytes 1572888
  2.7 0.0 copy-start.1
  2.7 1.4 %copy-done.1 = bf16[512,1536]{1,0:T(8,128)(2,1)S(1)} copy-done((bf16[512,1536]{1,0:T(8,128)(2,1)S(1)}, bf16[512,1536]{1,0:T(8,128)(2,1)}, u32[]{:S(2)}) %copy-start.1) | copy-done | bytes 1572888
  4.1 0.0 copy-start.2
  4.1 1.4 %copy-done.2 = bf16[512,1536]{1,0:T(8,128)(2,1)S(1)} copy-done((bf16[512,1536]{1,0:T(8,128)(2,1)S(1)}, bf16[512,1536]{1,0:T(8,128)(2,1)}, u32[]{:S(2)}) %copy-start.2) | copy-done | bytes 1572888
  5.5 0.0 copy-start.3
  5.5 0.7 %copy-done.3 = bf16[8,1536]{1,0:T(8,128)(2,1)S(1)} copy-done((bf16[8,1536]{1,0:T(8,128)(2,1)S(1)}, bf16[8,1536]{1,0:T(8,128)(2,1)}, u32[]{:S(2)}) %copy-start.3) | copy-done | bytes 24600
  6.2 0.0 copy-start.4
  6.2 0.7 %copy-done.4 = bf16[8,1536]{1,0:T(8,128)(2,1)S(1)} copy-done((bf16[8,1536]{1,0:T(8,128)(2,1)S(1)}, bf16[8,1536]{1,0:T(8,128)(2,1)}, u32[]{:S(2)}) %copy-start.4) | copy-done | bytes 24600
  7.0 0.0 copy-start.5
  7.0 0.7 %copy-done.5 = bf16[8,1536]{1,0:T(8,128)(2,1)S(1)} copy-done((bf16[8,1536]{1,0:T(8,128)(2,1)S(1)}, bf16[8,1536]{1,0:T(8,128)(2,1)}, u32[]{:S(2)}) %copy-start.5) | copy-done | bytes 24600
  7.7 0.0 copy-start.6
  7.7 0.7 %copy-done.6 = f32[128]{0:T(128)S(1)} copy-done((f32[128]{0:T(128)S(1)}, f32[128]{0:T(128)}, u32[]{:S(2)}) %copy-start.6) | copy-done | bytes 536
  8.4 0.0 copy-start.7
  8.4 0.7 %copy-done.7 = f32[128]{0:T(128)S(1)} copy-done((f32[128]{0:T(128)S(1)}, f32[128]{0:T(128)}, u32[]{:S(2)}) %copy-start.7) | copy-done | bytes 536
  9.0 0.0 copy-start.8
  9.0 0.7 %copy-done.8 = f32[128]{0:T(128)S(1)} copy-done((f32[128]{0:T(128)S(1)}, f32[128]{0:T(128)}, u32[]{:S(2)}) %copy-start.8) | copy-done | bytes 536
  9.7 0.0 copy-start.9
  9.7 0.7 %copy-done.9 = f32[128]{0:T(128)S(1)} copy-done((f32[128]{0:T(128)S(1)}, f32[128]{0:T(128)}, u32[]{:S(2)}) %copy-start.9) | copy-done | bytes 536
  10.3 0.0 copy-start.10
  10.3 0.7 %copy-done.10 = s32[8]{0:T(128)S(1)} copy-done((s32[8]{0:T(128)S(1)}, s32[8]{0:T(128)}, u32[]{:S(2)}) %copy-start.10) | copy-done | bytes 56
  11.0 16.1 %shard_map.131.parts_ref = bf16[4,40,384]{2,1,0:T(8,128)(2,1)S(1)} custom-call(bf16[8,1536]{1,0:T(8,128)(2,1)S(1)} %copy-done.3, bf16[8,1536]{1,0:T(8,128)(2,1)S(1)} %copy-done.4, bf16[8,1536]{1,0:T(8,128)(2,1)S(1)} %copy-done.5, bf16[512,1536]{1,0:T(8,128)(2,1)S(1)} %copy-done, bf16[512,1536]{1,0:T(8,128)(2,1)S(1)} %copy-done.1, ...), custom_call_target="tpu_custom_call" | custom-call | tf_op jit(solution)/shard_map/pallas_call | solution.py:325
  27.1 0.7 %shard_map.132 = (bf16[8,1536]{1,0:T(8,128)(2,1)}, bf16[32,1536]{1,0:T(8,128)(2,1)}) custom-call(bf16[4,40,384]{2,1,0:T(8,128)(2,1)S(1)} %shard_map.131.parts_ref), custom_call_target="tpu_custom_call" | custom-call | tf_op jit(solution)/shard_map/pallas_call | solution.py:363
Async XLA Ops:
  1.3 1.4 %copy-start = (bf16[512,1536]{1,0:T(8,128)(2,1)S(1)}, bf16[512,1536]{1,0:T(8,128)(2,1)}, u32[]{:S(2)}) copy-start(bf16[512,1536]{1,0:T(8,128)(2,1)} %tq_ref.1) | copy-start | bytes 4718596
  2.7 1.4 %copy-start.1 = (bf16[512,1536]{1,0:T(8,128)(2,1)S(1)}, bf16[512,1536]{1,0:T(8,128)(2,1)}, u32[]{:S(2)}) copy-start(bf16[512,1536]{1,0:T(8,128)(2,1)} %tk_ref.1) | copy-start | bytes 4718596
  4.1 1.4 %copy-start.2 = (bf16[512,1536]{1,0:T(8,128)(2,1)S(1)}, bf16[512,1536]{1,0:T(8,128)(2,1)}, u32[]{:S(2)}) copy-start(bf16[512,1536]{1,0:T(8,128)(2,1)} %tv_ref.1) | copy-start | bytes 4718596
  5.5 0.7 %copy-start.3 = (bf16[8,1536]{1,0:T(8,128)(2,1)S(1)}, bf16[8,1536]{1,0:T(8,128)(2,1)}, u32[]{:S(2)}) copy-start(bf16[8,1536]{1,0:T(8,128)(2,1)} %iq_ref.1) | copy-start | bytes 73732
  6.2 0.7 %copy-start.4 = (bf16[8,1536]{1,0:T(8,128)(2,1)S(1)}, bf16[8,1536]{1,0:T(8,128)(2,1)}, u32[]{:S(2)}) copy-start(bf16[8,1536]{1,0:T(8,128)(2,1)} %ik_ref.1) | copy-start | bytes 73732
  7.0 0.7 %copy-start.5 = (bf16[8,1536]{1,0:T(8,128)(2,1)S(1)}, bf16[8,1536]{1,0:T(8,128)(2,1)}, u32[]{:S(2)}) copy-start(bf16[8,1536]{1,0:T(8,128)(2,1)} %iv_ref.1) | copy-start | bytes 73732
  7.7 0.7 %copy-start.6 = (f32[128]{0:T(128)S(1)}, f32[128]{0:T(128)}, u32[]{:S(2)}) copy-start(f32[128]{0:T(128)} %param.18) | copy-start | bytes 1540
  8.4 0.7 %copy-start.7 = (f32[128]{0:T(128)S(1)}, f32[128]{0:T(128)}, u32[]{:S(2)}) copy-start(f32[128]{0:T(128)} %param.19) | copy-start | bytes 1540
  9.0 0.7 %copy-start.8 = (f32[128]{0:T(128)S(1)}, f32[128]{0:T(128)}, u32[]{:S(2)}) copy-start(f32[128]{0:T(128)} %param.20) | copy-start | bytes 1540
  9.7 0.7 %copy-start.9 = (f32[128]{0:T(128)S(1)}, f32[128]{0:T(128)}, u32[]{:S(2)}) copy-start(f32[128]{0:T(128)} %param.21) | copy-start | bytes 1540
  10.3 0.7 %copy-start.10 = (s32[8]{0:T(128)S(1)}, s32[8]{0:T(128)}, u32[]{:S(2)}) copy-start(s32[8]{0:T(128)} %order_ref.1) | copy-start | bytes 100

commit v2 on v1

--- a/solution.py
+++ b/solution.py
@@ -356,7 +356,7 @@
             pltpu.SemaphoreType.DMA((TEAM,)),
         ],
         compiler_params=pltpu.CompilerParams(
-            collective_id=0, has_side_effects=True, vmem_limit_bytes=32 * 1024 * 1024
+            collective_id=0, has_side_effects=True, vmem_limit_bytes=62 * 1024 * 1024
         ),
     )(iq, ik, iv, tq, tk, tv, *gains, order, length)
     parts = pltpu.with_memory_space_constraint(parts, pltpu.VMEM)

time: 28.2 us -> 18.2 us (0.65); the launches traced: 27.7 us -> 18 us
  local copies, waits for them, and re-layouts: 9.7 us -> 0 us
    unnamed x22 -> x0, local copies, waits for them, and re-layouts: 9.7 us -> none
where the time goes in v2:
time: 18.2 us; the launch traced here: 18 us
  Pallas kernels  16.7 us (92%)
  between operations  1.29 us (7%)
    pallas_call x1, Pallas kernels, local(): pl.pallas_call(functools.partial(kernel, devices), out_shape=pltpu.VMEM((...  16.1 us
    pallas_call x1, Pallas kernels, local(): pl.pallas_call(spread, out_shape=(jax.ShapeDtypeStruct((own_rows, width),...  0.65 us

profile of v2, /device:TPU:0, one launch (start us, length us, event | category | flops | bytes accessed | tf_op | source)
XLA Modules:
  0.0 18.0 jit_solution(10224780575160131141)
XLA Ops:
  1.3 16.1 %shard_map.131.parts_ref = bf16[4,40,384]{2,1,0:T(8,128)(2,1)S(1)} custom-call(bf16[8,1536]{1,0:T(8,128)(2,1)} %iq_ref.1, bf16[8,1536]{1,0:T(8,128)(2,1)} %ik_ref.1, bf16[8,1536]{1,0:T(8,128)(2,1)} %iv_ref.1, bf16[512,1536]{1,0:T(8,128)(2,1)} %tq_ref.1, bf16[512,1536]{1,0:T(8,128)(2,1)} %tk_ref.1, bf16[512,1536]{1,0:T(8,128)(2,1)} %tv_ref.1, ...), custom_call_target="tpu_custom_call" | custom-call | tf_op jit(solution)/shard_map/pallas_call | solution.py:325
  17.4 0.7 %shard_map.132 = (bf16[8,1536]{1,0:T(8,128)(2,1)}, bf16[32,1536]{1,0:T(8,128)(2,1)}) custom-call(bf16[4,40,384]{2,1,0:T(8,128)(2,1)S(1)} %shard_map.131.parts_ref), custom_call_target="tpu_custom_call" | custom-call | tf_op jit(solution)/shard_map/pallas_call | solution.py:363

commit v3 on v2

--- a/solution.py
+++ b/solution.py
@@ -56,6 +56,7 @@
     local_sem,
     kv_send,
     kv_recv,
+    ready_sem,
     q_send,
     q_recv,
     back_send,
@@ -68,10 +69,19 @@
     mates = [(team * TEAM + (seat ^ k), seat ^ k) for k in (3, 2, 1)]
 
     barrier = pltpu.get_barrier_semaphore()
-    for d in range(1, devices):
-        pl.semaphore_signal(
-            barrier, inc=1, device_id=(req, (me + d) % devices), device_id_type=MESH
-        )
+    teams = devices // TEAM
+    last = teams - 1
+    gate = teams - 2
+    for t in reversed(range(teams)):
+        direct = (team < last) | (t >= gate)
+        for k in (3, 2, 1, 0):
+            peer = t * TEAM + (seat ^ k)
+
+            @pl.when((peer != me) & direct)
+            def _():
+                pl.semaphore_signal(
+                    barrier, inc=1, device_id=(req, peer), device_id_type=MESH
+                )
 
     own_rows, width = iq_buf.shape
     size = gain_buf.shape[-1]
@@ -144,17 +154,10 @@
         key = turned(ik_buf[:, wide].astype(jnp.float32), gain_buf[0])
         both = jnp.concatenate([key, iv_buf[:, wide].astype(jnp.float32)], axis=0)
         kv_own[h // per, :, cols] = both.astype(jnp.bfloat16)
-    for i in (4, 5):
-        loads[i].wait()
-    for h in range(heads):
-        wide = slice(h * size, (h + 1) * size)
-        cols = slice(h % per * size, (h % per + 1) * size)
-        query = turned(iq_buf[:, wide].astype(jnp.float32), gain_buf[1])
-        q_own[h // per, :, cols] = query.astype(jnp.bfloat16)
-    kv_all[me] = kv_own[seat]
-    q_team[seat] = q_own[seat]
-
-    pl.semaphore_wait(barrier, devices - 1)
+
+    pl.semaphore_wait(
+        barrier, jnp.where(team < gate, devices - 1 - TEAM, devices - 1)
+    )
 
     def remote(src, dst, send, recv, peer):
         return pltpu.make_async_remote_copy(
@@ -189,16 +192,42 @@
             peer,
         )
 
-    for t in range(devices // TEAM):
+    @pl.when(team == gate)
+    def _():
+        for t in range(gate):
+            pl.semaphore_signal(
+                ready_sem, inc=1, device_id=(req, t * TEAM + seat), device_id_type=MESH
+            )
+
+    def feed(t, allowed):
         for k in (3, 2, 1, 0):
             peer = t * TEAM + (seat ^ k)
 
-            @pl.when(peer != me)
+            @pl.when((peer != me) & allowed)
             def _():
                 kv_copy(peer, me).start()
 
+    for t in range(last):
+        feed(t, True)
+    feed(last, team >= gate)
+
+    for i in (4, 5):
+        loads[i].wait()
+    for h in range(heads):
+        wide = slice(h * size, (h + 1) * size)
+        cols = slice(h % per * size, (h % per + 1) * size)
+        query = turned(iq_buf[:, wide].astype(jnp.float32), gain_buf[1])
+        q_own[h // per, :, cols] = query.astype(jnp.bfloat16)
     for peer, mate in mates:
         q_copy(peer, mate, seat).start()
+    kv_all[me] = kv_own[seat]
+    q_team[seat] = q_own[seat]
+
+    @pl.when(team < gate)
+    def _():
+        pl.semaphore_wait(ready_sem, 1)
+
+    feed(last, team < gate)
 
     for i in range(6, 12):
         loads[i].wait()
@@ -247,8 +276,13 @@
         qs[h, team_text:] = query
         text_part(h, slice(team_text, team_rows), query)
 
-    for d in range(1, devices):
-        kv_copy(me, (me + d) % devices).wait_recv()
+    for t in range(teams):
+        for k in (0, 1, 2, 3):
+            origin = t * TEAM + (seat ^ k)
+
+            @pl.when(origin != me)
+            def _():
+                kv_copy(me, origin).wait_recv()
 
     def gathered(start, h):
         cols = slice(h * size, (h + 1) * size)
@@ -285,17 +319,22 @@
                 axis=0,
             )
             back_own[s, :, cols] = part.astype(jnp.bfloat16)
-    for peer, mate in mates:
-        back_copy(peer, mate, seat).start()
+    for mate in range(TEAM):
+
+        @pl.when(mate != seat)
+        def _():
+            back_copy(team * TEAM + mate, mate, seat).start()
+
     back_all[seat] = back_own[seat]
-    for peer, mate in mates:
-        back_copy(me, mate, mate).wait_recv()
-    out_ref[...] = back_all[...]
-
     for d in range(1, devices):
         kv_copy((me + d) % devices, me).wait_send()
     for peer, mate in mates:
         q_copy(peer, mate, seat).wait_send()
+    for peer, mate in mates:
+        back_copy(me, mate, mate).wait_recv()
+    out_ref[...] = back_all[...]
+
+    for peer, mate in mates:
         back_copy(peer, mate, seat).wait_send()
 
 
@@ -350,6 +389,7 @@
             pltpu.SemaphoreType.DMA((12,)),
             pltpu.SemaphoreType.DMA((devices,)),
             pltpu.SemaphoreType.DMA((devices,)),
+            pltpu.SemaphoreType.REGULAR,
             pltpu.SemaphoreType.DMA((TEAM,)),
             pltpu.SemaphoreType.DMA((TEAM,)),
             pltpu.SemaphoreType.DMA((TEAM,)),

time: 18.2 us -> 17.5 us (0.962)
  Pallas kernels: 16.7 us -> 16.1 us
    pallas_call x1, Pallas kernels: 16.1 us -> 15.4 us  [local(): pl.pallas_call(functools.partial(kernel, devices), out_shape=pltpu.VMEM((...]
where the time goes in v3:
time: 17.5 us; the launch traced here: 17.4 us
  Pallas kernels  16.1 us (92%)
  between operations  1.29 us (7%)
    pallas_call x1, Pallas kernels, local(): pl.pallas_call(functools.partial(kernel, devices), out_shape=pltpu.VMEM((...  15.4 us
    pallas_call x1, Pallas kernels, local(): pl.pallas_call(spread, out_shape=(jax.ShapeDtypeStruct((own_rows, width),...  0.65 us

profile of v3, /device:TPU:0, one launch (start us, length us, event | category | flops | bytes accessed | tf_op | source)
XLA Modules:
  0.0 17.4 jit_solution(1820858021247789978)
XLA Ops:
  1.3 15.4 %shard_map.131.parts_ref = bf16[4,40,384]{2,1,0:T(8,128)(2,1)S(1)} custom-call(bf16[8,1536]{1,0:T(8,128)(2,1)} %iq_ref.1, bf16[8,1536]{1,0:T(8,128)(2,1)} %ik_ref.1, bf16[8,1536]{1,0:T(8,128)(2,1)} %iv_ref.1, bf16[512,1536]{1,0:T(8,128)(2,1)} %tq_ref.1, bf16[512,1536]{1,0:T(8,128)(2,1)} %tk_ref.1, bf16[512,1536]{1,0:T(8,128)(2,1)} %tv_ref.1, ...), custom_call_target="tpu_custom_call" | custom-call | tf_op jit(solution)/shard_map/pallas_call | solution.py:364
  16.7 0.7 %shard_map.132 = (bf16[8,1536]{1,0:T(8,128)(2,1)}, bf16[32,1536]{1,0:T(8,128)(2,1)}) custom-call(bf16[4,40,384]{2,1,0:T(8,128)(2,1)S(1)} %shard_map.131.parts_ref), custom_call_target="tpu_custom_call" | custom-call | tf_op jit(solution)/shard_map/pallas_call | solution.py:403

commit v4 on v3

--- a/solution.py
+++ b/solution.py
@@ -12,6 +12,7 @@
 EPS = 1e-06
 LOW = -1e30
 TEAM = 4
+ORDERS = ((3, 2, 1, 0), (3, 2, 1, 0), (3, 1, 2, 0), (3, 2, 1, 0))
 MESH = pl.DeviceIdType.MESH
 
 
@@ -71,13 +72,11 @@
     barrier = pltpu.get_barrier_semaphore()
     teams = devices // TEAM
     last = teams - 1
-    gate = teams - 2
     for t in reversed(range(teams)):
-        direct = (team < last) | (t >= gate)
         for k in (3, 2, 1, 0):
             peer = t * TEAM + (seat ^ k)
 
-            @pl.when((peer != me) & direct)
+            @pl.when((peer != me) & (t >= team))
             def _():
                 pl.semaphore_signal(
                     barrier, inc=1, device_id=(req, peer), device_id_type=MESH
@@ -155,9 +154,7 @@
         both = jnp.concatenate([key, iv_buf[:, wide].astype(jnp.float32)], axis=0)
         kv_own[h // per, :, cols] = both.astype(jnp.bfloat16)
 
-    pl.semaphore_wait(
-        barrier, jnp.where(team < gate, devices - 1 - TEAM, devices - 1)
-    )
+    pl.semaphore_wait(barrier, (team + 1) * TEAM - 1)
 
     def remote(src, dst, send, recv, peer):
         return pltpu.make_async_remote_copy(
@@ -192,24 +189,42 @@
             peer,
         )
 
-    @pl.when(team == gate)
-    def _():
-        for t in range(gate):
+    for t in range(last):
+
+        @pl.when(t < team)
+        def _():
             pl.semaphore_signal(
-                ready_sem, inc=1, device_id=(req, t * TEAM + seat), device_id_type=MESH
+                ready_sem.at[team],
+                inc=1,
+                device_id=(req, t * TEAM + seat),
+                device_id_type=MESH,
             )
 
+    def pick(values):
+        value = values[-1]
+        for place in reversed(range(TEAM - 1)):
+            value = jnp.where(seat == place, values[place], value)
+        return value
+
+    places = [pick(column) for column in zip(*ORDERS)]
+
     def feed(t, allowed):
-        for k in (3, 2, 1, 0):
-            peer = t * TEAM + (seat ^ k)
+        for place in places:
+            peer = t * TEAM + place
 
             @pl.when((peer != me) & allowed)
             def _():
                 kv_copy(peer, me).start()
 
-    for t in range(last):
-        feed(t, True)
-    feed(last, team >= gate)
+    for t in range(teams):
+        feed(t, t <= team)
+
+    def feed_later(t):
+        @pl.when(team < t)
+        def _():
+            pl.semaphore_wait(ready_sem.at[t], 1)
+
+        feed(t, team < t)
 
     for i in (4, 5):
         loads[i].wait()
@@ -222,12 +237,9 @@
         q_copy(peer, mate, seat).start()
     kv_all[me] = kv_own[seat]
     q_team[seat] = q_own[seat]
-
-    @pl.when(team < gate)
-    def _():
-        pl.semaphore_wait(ready_sem, 1)
-
-    feed(last, team < gate)
+    for t in range(1, last):
+        feed_later(t)
+
 
     for i in range(6, 12):
         loads[i].wait()
@@ -266,6 +278,9 @@
         query = (query * rsqrt_mean(query) * gain_buf[3]).astype(jnp.bfloat16)
         qs[h, :team_text] = query
         text_part(h, slice(0, team_text), query)
+
+        if h == 0:
+            feed_later(last)
 
     for peer, mate in mates:
         q_copy(me, mate, mate).wait_recv()
@@ -357,6 +372,7 @@
     share = text_rows // devices
     team_text = share * TEAM
     team_rows = team_text + TEAM * own_rows
+    teams = devices // TEAM
     vmem = pl.BlockSpec(memory_space=pltpu.VMEM)
     hbm = pl.BlockSpec(memory_space=pl.ANY)
     gains = [g.reshape(1, size) for g in (iqg, ikg, tqg, tkg)]
@@ -389,7 +405,7 @@
             pltpu.SemaphoreType.DMA((12,)),
             pltpu.SemaphoreType.DMA((devices,)),
             pltpu.SemaphoreType.DMA((devices,)),
-            pltpu.SemaphoreType.REGULAR,
+            pltpu.SemaphoreType.REGULAR((teams,)),
             pltpu.SemaphoreType.DMA((TEAM,)),
             pltpu.SemaphoreType.DMA((TEAM,)),
             pltpu.SemaphoreType.DMA((TEAM,)),

time: 17.5 us -> 16.8 us (0.960)
  Pallas kernels: 16.1 us -> 15.4 us
    pallas_call x1, Pallas kernels: 15.4 us -> 14.7 us  [local(): pl.pallas_call(functools.partial(kernel, devices), out_shape=pltpu.VMEM((...]
where the time goes in v4:
time: 16.8 us; the launch traced here: 16.6 us
  Pallas kernels  15.4 us (92%)
  between operations  1.29 us (8%)
    pallas_call x1, Pallas kernels, local(): pl.pallas_call(functools.partial(kernel, devices), out_shape=pltpu.VMEM((...  14.7 us
    pallas_call x1, Pallas kernels, local(): pl.pallas_call(spread, out_shape=(jax.ShapeDtypeStruct((own_rows, width),...  0.65 us

profile of v4, /device:TPU:0, one launch (start us, length us, event | category | flops | bytes accessed | tf_op | source)
XLA Modules:
  0.0 16.6 jit_solution(14470608480588639727)
XLA Ops:
  1.3 14.7 %shard_map.131.parts_ref = bf16[4,40,384]{2,1,0:T(8,128)(2,1)S(1)} custom-call(bf16[8,1536]{1,0:T(8,128)(2,1)} %iq_ref.1, bf16[8,1536]{1,0:T(8,128)(2,1)} %ik_ref.1, bf16[8,1536]{1,0:T(8,128)(2,1)} %iv_ref.1, bf16[512,1536]{1,0:T(8,128)(2,1)} %tq_ref.1, bf16[512,1536]{1,0:T(8,128)(2,1)} %tk_ref.1, bf16[512,1536]{1,0:T(8,128)(2,1)} %tv_ref.1, ...), custom_call_target="tpu_custom_call" | custom-call | tf_op jit(solution)/shard_map/pallas_call | solution.py:380
  16.0 0.7 %shard_map.132 = (bf16[8,1536]{1,0:T(8,128)(2,1)}, bf16[32,1536]{1,0:T(8,128)(2,1)}) custom-call(bf16[4,40,384]{2,1,0:T(8,128)(2,1)S(1)} %shard_map.131.parts_ref), custom_call_target="tpu_custom_call" | custom-call | tf_op jit(solution)/shard_map/pallas_call | solution.py:419

commit v5 on v4

--- a/solution.py
+++ b/solution.py
@@ -12,7 +12,8 @@
 EPS = 1e-06
 LOW = -1e30
 TEAM = 4
-ORDERS = ((3, 2, 1, 0), (3, 2, 1, 0), (3, 1, 2, 0), (3, 2, 1, 0))
+MAKERS = 3
+ORDERS = ((2, 1, 0), (2, 1, 0), (1, 2, 0), (1, 2, 0))
 MESH = pl.DeviceIdType.MESH
 
 
@@ -34,7 +35,8 @@
     tkg_ref,
     order_ref,
     length_ref,
-    out_ref,
+    image_out_ref,
+    text_out_ref,
     iq_buf,
     ik_buf,
     iv_buf,
@@ -67,7 +69,6 @@
     req = lax.axis_index("req")
     seat = me % TEAM
     team = me // TEAM
-    mates = [(team * TEAM + (seat ^ k), seat ^ k) for k in (3, 2, 1)]
 
     barrier = pltpu.get_barrier_semaphore()
     teams = devices // TEAM
@@ -92,7 +93,9 @@
     team_rows = team_text + TEAM * own_rows
     scale = math.log2(math.e) / math.sqrt(size)
 
-    lanes = pl.ds(pl.multiple_of(seat * span, span), span)
+    makes = seat < MAKERS
+    part = jnp.minimum(seat, MAKERS - 1)
+    lanes = pl.ds(pl.multiple_of(part * span, span), span)
     text = pl.ds(pl.multiple_of(team * team_text, team_text), team_text)
     loads = []
     for src, dst in (
@@ -175,19 +178,27 @@
             peer,
         )
 
-    def q_copy(peer, mate, origin):
+    def q_copy(mate):
         return remote(
-            q_own.at[mate], q_team.at[origin], q_send.at[mate], q_recv.at[origin], peer
-        )
-
-    def back_copy(peer, mate, origin):
+            q_own.at[mate],
+            q_team.at[seat],
+            q_send.at[mate],
+            q_recv.at[seat],
+            team * TEAM + mate,
+        )
+
+    def back_copy(mate):
         return remote(
             back_own.at[mate],
-            back_all.at[origin],
+            back_all.at[part],
             back_send.at[mate],
-            back_recv.at[origin],
-            peer,
-        )
+            back_recv.at[part],
+            team * TEAM + mate,
+        )
+
+    def arrive(buf, sends, arrivals, origin):
+        here = buf.at[origin]
+        remote(here, here, sends.at[0], arrivals.at[origin], me).wait_recv()
 
     for t in range(last):
 
@@ -233,11 +244,15 @@
         cols = slice(h % per * size, (h % per + 1) * size)
         query = turned(iq_buf[:, wide].astype(jnp.float32), gain_buf[1])
         q_own[h // per, :, cols] = query.astype(jnp.bfloat16)
-    for peer, mate in mates:
-        q_copy(peer, mate, seat).start()
-    kv_all[me] = kv_own[seat]
-    q_team[seat] = q_own[seat]
-    for t in range(1, last):
+    for mate in reversed(range(MAKERS)):
+
+        @pl.when(mate != seat)
+        def _():
+            q_copy(mate).start()
+
+    kv_all[me] = kv_own[part]
+    q_team[seat] = q_own[part]
+    for t in range(1, teams):
         feed_later(t)
 
 
@@ -270,103 +285,125 @@
             preferred_element_type=jnp.float32,
         )
 
-    for h in range(per):
-        cols = slice(h * size, (h + 1) * size)
-        key = tk_buf[:, cols].astype(jnp.float32)
-        tk_buf[:, cols] = (key * rsqrt_mean(key) * gain_buf[2]).astype(jnp.bfloat16)
-        query = tq_buf[:, cols].astype(jnp.float32)
-        query = (query * rsqrt_mean(query) * gain_buf[3]).astype(jnp.bfloat16)
-        qs[h, :team_text] = query
-        text_part(h, slice(0, team_text), query)
-
-        if h == 0:
-            feed_later(last)
-
-    for peer, mate in mates:
-        q_copy(me, mate, mate).wait_recv()
-    for h in range(per):
-        cols = slice(h * size, (h + 1) * size)
-        query = q_team[:, :, cols].astype(jnp.float32)
-        query = query.reshape(TEAM * own_rows, size).astype(jnp.bfloat16)
-        qs[h, team_text:] = query
-        text_part(h, slice(team_text, team_rows), query)
-
-    for t in range(teams):
-        for k in (0, 1, 2, 3):
-            origin = t * TEAM + (seat ^ k)
-
-            @pl.when(origin != me)
-            def _():
-                kv_copy(me, origin).wait_recv()
-
     def gathered(start, h):
         cols = slice(h * size, (h + 1) * size)
-        whole = kv_all[:, start : start + own_rows, cols].astype(jnp.float32)
-        return whole.reshape(devices * own_rows, size).astype(jnp.bfloat16)
-
-    every = range(per)
-    scores = [scores_of(qs[h], gathered(0, h)) for h in every]
-    olds = [m_buf[h] for h in every]
-    tops = [
-        jnp.maximum(olds[h][:, :1], jnp.max(scores[h], axis=-1, keepdims=True))
-        for h in every
+        whole = kv_all[:, start : start + own_rows, cols]
+        return whole.reshape(devices * own_rows, size)
+
+    @pl.when(makes)
+    def _():
+        for h in range(per):
+            cols = slice(h * size, (h + 1) * size)
+            key = tk_buf[:, cols].astype(jnp.float32)
+            tk_buf[:, cols] = (key * rsqrt_mean(key) * gain_buf[2]).astype(jnp.bfloat16)
+            query = tq_buf[:, cols].astype(jnp.float32)
+            query = (query * rsqrt_mean(query) * gain_buf[3]).astype(jnp.bfloat16)
+            qs[h, :team_text] = query
+            text_part(h, slice(0, team_text), query)
+
+        for k in (3, 2, 1):
+            arrive(q_team, q_send, q_recv, seat ^ k)
+        for h in range(per):
+            cols = slice(h * size, (h + 1) * size)
+            query = q_team[:, :, cols].astype(jnp.float32)
+            query = query.reshape(TEAM * own_rows, size).astype(jnp.bfloat16)
+            qs[h, team_text:] = query
+            text_part(h, slice(team_text, team_rows), query)
+
+        for t in range(teams):
+            for k in (0, 1, 2, 3):
+                origin = t * TEAM + (seat ^ k)
+
+                @pl.when(origin != me)
+                def _():
+                    arrive(kv_all, kv_send, kv_recv, origin)
+
+        every = range(per)
+        scores = [scores_of(qs[h], gathered(0, h)) for h in every]
+        olds = [m_buf[h] for h in every]
+        tops = [
+            jnp.maximum(olds[h][:, :1], jnp.max(scores[h], axis=-1, keepdims=True))
+            for h in every
+        ]
+        expos = [jnp.exp2(scores[h] - tops[h]) for h in every]
+        added = [
+            jnp.dot(
+                expos[h].astype(jnp.bfloat16),
+                gathered(own_rows, h),
+                preferred_element_type=jnp.float32,
+            )
+            for h in every
+        ]
+        sums = [jnp.sum(expos[h], axis=-1, keepdims=True) for h in every]
+        for h in every:
+            cols = slice(h * size, (h + 1) * size)
+            back = jnp.exp2(olds[h] - tops[h])
+            out = (o_buf[h] * back + added[h]) / (l_buf[h] * back + sums[h])
+            for s in range(TEAM):
+                rows = jnp.concatenate(
+                    [
+                        out[s * share : (s + 1) * share],
+                        out[team_text + s * own_rows : team_text + (s + 1) * own_rows],
+                    ],
+                    axis=0,
+                )
+                back_own[s, :, cols] = rows.astype(jnp.bfloat16)
+        for mate in range(TEAM):
+
+            @pl.when(mate != seat)
+            def _():
+                back_copy(mate).start()
+
+        back_all[seat] = back_own[seat]
+
+    for t in range(teams):
+        for place in range(MAKERS):
+            peer = t * TEAM + place
+
+            @pl.when(peer != me)
+            def _():
+                kv_copy(peer, me).wait_send()
+
+    for mate in range(MAKERS):
+
+        @pl.when(mate != seat)
+        def _():
+            q_copy(mate).wait_send()
+
+    for origin in reversed(range(MAKERS)):
+
+        @pl.when(origin != seat)
+        def _():
+            arrive(back_all, back_send, back_recv, origin)
+
+    for place in range(MAKERS):
+        cols = slice(place * span, (place + 1) * span)
+        text_out_ref[:, cols] = back_all[place, :share]
+        image_out_ref[:, cols] = back_all[place, share:]
+
+    for mate in range(TEAM):
+
+        @pl.when(makes & (mate != seat))
+        def _():
+            back_copy(mate).wait_send()
+
+
+def store(image_ref, text_ref, io_ref, to_ref, sems):
+    copies = [
+        pltpu.make_async_copy(image_ref, io_ref, sems.at[0]),
+        pltpu.make_async_copy(text_ref, to_ref, sems.at[1]),
     ]
-    expos = [jnp.exp2(scores[h] - tops[h]) for h in every]
-    added = [
-        jnp.dot(
-            expos[h].astype(jnp.bfloat16),
-            gathered(own_rows, h),
-            preferred_element_type=jnp.float32,
-        )
-        for h in every
-    ]
-    sums = [jnp.sum(expos[h], axis=-1, keepdims=True) for h in every]
-    for h in every:
-        cols = slice(h * size, (h + 1) * size)
-        back = jnp.exp2(olds[h] - tops[h])
-        out = (o_buf[h] * back + added[h]) / (l_buf[h] * back + sums[h])
-        for s in range(TEAM):
-            part = jnp.concatenate(
-                [
-                    out[s * share : (s + 1) * share],
-                    out[team_text + s * own_rows : team_text + (s + 1) * own_rows],
-                ],
-                axis=0,
-            )
-            back_own[s, :, cols] = part.astype(jnp.bfloat16)
-    for mate in range(TEAM):
-
-        @pl.when(mate != seat)
-        def _():
-            back_copy(team * TEAM + mate, mate, seat).start()
-
-    back_all[seat] = back_own[seat]
-    for d in range(1, devices):
-        kv_copy((me + d) % devices, me).wait_send()
-    for peer, mate in mates:
-        q_copy(peer, mate, seat).wait_send()
-    for peer, mate in mates:
-        back_copy(me, mate, mate).wait_recv()
-    out_ref[...] = back_all[...]
-
-    for peer, mate in mates:
-        back_copy(peer, mate, seat).wait_send()
-
-
-def spread(parts_ref, io_ref, to_ref):
-    share = to_ref.shape[0]
-    span = parts_ref.shape[-1]
-    for s in range(TEAM):
-        cols = slice(s * span, (s + 1) * span)
-        to_ref[:, cols] = parts_ref[s, :share]
-        io_ref[:, cols] = parts_ref[s, share:]
+    for copy in copies:
+        copy.start()
+    for copy in copies:
+        copy.wait()
 
 
 def local(iq, ik, iv, tq, tk, tv, iqg, ikg, tqg, tkg, order, length):
     devices = lax.axis_size("seq")
     own_rows, width = iq.shape
     size = iqg.shape[0]
-    span = width // TEAM
+    span = width // MAKERS
     per = span // size
     text_rows = tq.shape[0]
     share = text_rows // devices
@@ -379,9 +416,12 @@
     bf16, f32 = jnp.bfloat16, jnp.float32
     parts = pl.pallas_call(
         functools.partial(kernel, devices),
-        out_shape=pltpu.VMEM((TEAM, share + own_rows, span), bf16),
+        out_shape=(
+            pltpu.VMEM((own_rows, width), bf16),
+            pltpu.VMEM((share, width), bf16),
+        ),
         in_specs=[hbm] * 12,
-        out_specs=vmem,
+        out_specs=(vmem, vmem),
         scratch_shapes=[
             pltpu.VMEM((own_rows, width), bf16),
             pltpu.VMEM((own_rows, width), bf16),
@@ -392,8 +432,8 @@
             pltpu.VMEM((4, 1, size), f32),
             pltpu.SMEM((own_rows,), jnp.int32),
             pltpu.SMEM((1,), jnp.int32),
-            pltpu.VMEM((TEAM, 2 * own_rows, span), bf16),
-            pltpu.VMEM((TEAM, own_rows, span), bf16),
+            pltpu.VMEM((MAKERS, 2 * own_rows, span), bf16),
+            pltpu.VMEM((MAKERS, own_rows, span), bf16),
             pltpu.VMEM((devices, 2 * own_rows, span), bf16),
             pltpu.VMEM((TEAM, own_rows, span), bf16),
             pltpu.VMEM((per, team_rows, size), bf16),
@@ -401,7 +441,7 @@
             pltpu.VMEM((per, team_rows, size), f32),
             pltpu.VMEM((per, team_rows, size), f32),
             pltpu.VMEM((TEAM, share + own_rows, span), bf16),
-            pltpu.VMEM((TEAM, share + own_rows, span), bf16),
+            pltpu.VMEM((MAKERS, share + own_rows, span), bf16),
             pltpu.SemaphoreType.DMA((12,)),
             pltpu.SemaphoreType.DMA((devices,)),
             pltpu.SemaphoreType.DMA((devices,)),
@@ -415,16 +455,17 @@
             collective_id=0, has_side_effects=True, vmem_limit_bytes=62 * 1024 * 1024
         ),
     )(iq, ik, iv, tq, tk, tv, *gains, order, length)
-    parts = pltpu.with_memory_space_constraint(parts, pltpu.VMEM)
+    parts = [pltpu.with_memory_space_constraint(p, pltpu.VMEM) for p in parts]
     return pl.pallas_call(
-        spread,
+        store,
         out_shape=(
             jax.ShapeDtypeStruct((own_rows, width), bf16),
             jax.ShapeDtypeStruct((share, width), bf16),
         ),
-        in_specs=[vmem],
-        out_specs=(vmem, vmem),
-    )(parts)
+        in_specs=[vmem, vmem],
+        out_specs=(hbm, hbm),
+        scratch_shapes=[pltpu.SemaphoreType.DMA((2,))],
+    )(*parts)
 
 
 def solution(mesh):

time: 16.8 us -> 16.8 us (level)
  no operation moved by 1% of the time
where the time goes in v5:
time: 16.8 us; the launch traced here: 16.6 us
  Pallas kernels  15.3 us (91%)
  between operations  1.29 us (8%)
    pallas_call x1, Pallas kernels, local(): pl.pallas_call(functools.partial(kernel, devices), out_shape=(pltpu.VMEM(...  14.6 us
    pallas_call x1, Pallas kernels, local(): pl.pallas_call(store, out_shape=(jax.ShapeDtypeStruct((own_rows, width),...  0.67 us

profile of v5, /device:TPU:0, one launch (start us, length us, event | category | flops | bytes accessed | tf_op | source)
XLA Modules:
  0.0 16.6 jit_solution(15307025016349847111)
XLA Ops:
  1.3 14.6 %shard_map.131 = (bf16[8,1536]{1,0:T(8,128)(2,1)S(1)}, bf16[32,1536]{1,0:T(8,128)(2,1)S(1)}) custom-call(bf16[8,1536]{1,0:T(8,128)(2,1)} %iq_ref.1, bf16[8,1536]{1,0:T(8,128)(2,1)} %ik_ref.1, bf16[8,1536]{1,0:T(8,128)(2,1)} %iv_ref.1, bf16[512,1536]{1,0:T(8,128)(2,1)} %tq_ref.1, bf16[512,1536]{1,0:T(8,128)(2,1)} %tk_ref.1, bf16[512,1536]{1,0:T(8,128)(2,1)} %tv_ref.1, ...), custom_call_target="tpu_custom_call" | custom-call | tf_op jit(solution)/shard_map/pallas_call | solution.py:417
  15.9 0.7 %shard_map.132 = (bf16[8,1536]{1,0:T(8,128)(2,1)}, bf16[32,1536]{1,0:T(8,128)(2,1)}) custom-call(bf16[8,1536]{1,0:T(8,128)(2,1)S(1)} %get-tuple-element.4.image_ref, bf16[32,1536]{1,0:T(8,128)(2,1)S(1)} %get-tuple-element.5.text_ref), custom_call_target="tpu_custom_call" | custom-call | tf_op jit(solution)/shard_map/pallas_call | solution.py:459

commit v6 on v5

--- a/solution.py
+++ b/solution.py
@@ -227,8 +227,7 @@
             def _():
                 kv_copy(peer, me).start()
 
-    for t in range(teams):
-        feed(t, t <= team)
+    feed(0, True)
 
     def feed_later(t):
         @pl.when(team < t)
@@ -252,6 +251,8 @@
 
     kv_all[me] = kv_own[part]
     q_team[seat] = q_own[part]
+    for t in range(1, teams):
+        feed(t, t <= team)
     for t in range(1, teams):
         feed_later(t)
 

time: 16.8 us -> 16.8 us (level)
  no operation moved by 1% of the time
where the time goes in v6:
time: 16.8 us; the launch traced here: 16.6 us
  Pallas kernels  15.3 us (91%)
  between operations  1.29 us (8%)
    pallas_call x1, Pallas kernels, local(): pl.pallas_call(functools.partial(kernel, devices), out_shape=(pltpu.VMEM(...  14.6 us
    pallas_call x1, Pallas kernels, local(): pl.pallas_call(store, out_shape=(jax.ShapeDtypeStruct((own_rows, width),...  0.67 us

profile of v6, /device:TPU:0, one launch (start us, length us, event | category | flops | bytes accessed | tf_op | source)
XLA Modules:
  0.0 16.6 jit_solution(17921022068524147814)
XLA Ops:
  1.3 14.6 %shard_map.131 = (bf16[8,1536]{1,0:T(8,128)(2,1)S(1)}, bf16[32,1536]{1,0:T(8,128)(2,1)S(1)}) custom-call(bf16[8,1536]{1,0:T(8,128)(2,1)} %iq_ref.1, bf16[8,1536]{1,0:T(8,128)(2,1)} %ik_ref.1, bf16[8,1536]{1,0:T(8,128)(2,1)} %iv_ref.1, bf16[512,1536]{1,0:T(8,128)(2,1)} %tq_ref.1, bf16[512,1536]{1,0:T(8,128)(2,1)} %tk_ref.1, bf16[512,1536]{1,0:T(8,128)(2,1)} %tv_ref.1, ...), custom_call_target="tpu_custom_call" | custom-call | tf_op jit(solution)/shard_map/pallas_call | solution.py:418
  15.9 0.7 %shard_map.132 = (bf16[8,1536]{1,0:T(8,128)(2,1)}, bf16[32,1536]{1,0:T(8,128)(2,1)}) custom-call(bf16[8,1536]{1,0:T(8,128)(2,1)S(1)} %get-tuple-element.4.image_ref, bf16[32,1536]{1,0:T(8,128)(2,1)S(1)} %get-tuple-element.5.text_ref), custom_call_target="tpu_custom_call" | custom-call | tf_op jit(solution)/shard_map/pallas_call | solution.py:460
